TPU v7x, 32 devices: a whole 2x2x4 slice. The times are simulated.
32 devices in a mesh: depth: 4 (over z), rows: 8 (over y, x, core).
Axes of the slice: x: 2, y: 2, z: 4, core: 2. Of those that a mesh axis runs over, the one named last changes fastest.
Arguments:
- target: float32 [4, 2, 4096, 4096], P('depth', None, 'rows'), may hold values from -6 to 6
- depth_index: int32 [4], P('depth'), may hold values from 0 to 255
- band_mask: int32 [4, 2, 4096], P('depth'), may hold values from 0 to 1, as said below
Outputs:
- hologram: float32 [2, 4096, 4096], P(None, ('depth', 'rows'))
Inputs may be any that keep to these rules, and one draw needn't show every extreme that they name: `band_mask`: for each plane and each of the two dimensions, the ones are exactly the frequency indices k with min(k, 4096 - k) below a cutoff between 512 and 2048.
All inputs are finite; a program needn't handle non-finite values.
Results may differ from a plain program's by a relative error of at most 0.0009.
Values sent between devices are 32-bit elements; how exact they have to be, the bound alone decides.
A program may use at most 128 MiB of HBM per device.

v0:
```python
import math
import jax
import jax.numpy as jnp
from jax import lax
from jax.sharding import PartitionSpec as P

LOW = 32
HIGH = 128
N = 4096
precise = lax.Precision.HIGHEST


def block_table(length, direction):
    indices = jnp.arange(length, dtype=jnp.int32)
    product = indices[:, None] * indices[None, :] % length
    angles = direction * 2.0 * math.pi / length * product.astype(jnp.float32)
    cosine = jnp.cos(angles)
    sine_part = jnp.sin(angles)
    upper_rows = jnp.stack([cosine, -sine_part], axis=1)
    lower_rows = jnp.stack([sine_part, cosine], axis=1)
    return jnp.stack([upper_rows, lower_rows], axis=0)


def twiddles(direction):
    first = jnp.arange(LOW, dtype=jnp.int32)
    second = jnp.arange(HIGH, dtype=jnp.int32)
    product = first[:, None] * second[None, :] % N
    angles = direction * 2.0 * math.pi / N * product.astype(jnp.float32)
    scaling = 1.0 / math.sqrt(N)
    return (jnp.cos(angles) * scaling, jnp.sin(angles) * scaling)


def rotate_pair(data, factor_real, factor_imaginary, comp_axis):
    real_part = jnp.take(data, 0, axis=comp_axis)
    imaginary_part = jnp.take(data, 1, axis=comp_axis)
    return jnp.stack(
        [
            real_part * factor_real - imaginary_part * factor_imaginary,
            real_part * factor_imaginary + imaginary_part * factor_real,
        ],
        axis=comp_axis,
    )


def along_width(planes):
    plane_count, _, height, _ = planes.shape
    factor_real, factor_imaginary = twiddles(-1.0)
    pieces = planes.reshape(plane_count, 2, height, LOW, HIGH)
    sectioned = jnp.einsum("akbn,pbrnm->parkm", block_table(LOW, -1.0), pieces, precision=precise)
    turned = rotate_pair(sectioned, factor_real, factor_imaginary, 1)
    result = jnp.einsum("akbn,pbrjn->parjk", block_table(HIGH, -1.0), turned, precision=precise)
    return result.reshape(plane_count, 2, height, N)


def along_height(columns):
    plane_count, _, _, slab_width = columns.shape
    factor_real, factor_imaginary = twiddles(-1.0)
    pieces = columns.reshape(plane_count, 2, LOW, HIGH, slab_width)
    sectioned = jnp.einsum("akbn,pbnjs->pakjs", block_table(LOW, -1.0), pieces, precision=precise)
    turned = rotate_pair(sectioned, factor_real[:, :, None], factor_imaginary[:, :, None], 1)
    result = jnp.einsum("akbn,pbjns->pajks", block_table(HIGH, -1.0), turned, precision=precise)
    return result.reshape(plane_count, 2, N, slab_width)


def inverse_height(spectrum):
    slab_width = spectrum.shape[2]
    factor_real, factor_imaginary = twiddles(1.0)
    pieces = spectrum.reshape(2, LOW, HIGH, slab_width)
    sectioned = jnp.einsum("anbk,bjks->ajns", block_table(HIGH, 1.0), pieces, precision=precise)
    turned = rotate_pair(sectioned, factor_real[:, :, None], factor_imaginary[:, :, None], 0)
    result = jnp.einsum("anbk,bkjs->anjs", block_table(LOW, 1.0), turned, precision=precise)
    return result.reshape(2, N, slab_width)


def inverse_width(row_block):
    height = row_block.shape[1]
    factor_real, factor_imaginary = twiddles(1.0)
    pieces = row_block.reshape(2, height, LOW, HIGH)
    sectioned = jnp.einsum("anbk,byjk->ayjn", block_table(HIGH, 1.0), pieces, precision=precise)
    turned = rotate_pair(sectioned, factor_real, factor_imaginary, 0)
    result = jnp.einsum("anbk,bykj->aynj", block_table(LOW, 1.0), turned, precision=precise)
    return result.reshape(2, height, N)


def frequencies(ordering):
    first = ordering // HIGH
    second = ordering % HIGH
    natural = first + LOW * second
    signed = jnp.where(natural < N // 2, natural, natural - N)
    return signed.astype(jnp.float32) / N


def reorder_mask(band_mask):
    leading = band_mask.shape[:-1]
    grid = band_mask.reshape(leading + (HIGH, LOW))
    return jnp.swapaxes(grid, -1, -2).reshape(leading + (N,))


def local(target, depth_index, band_mask):
    plane_count = target.shape[0]
    spectra_width = along_width(target)
    columns = along_height(
        lax.all_to_all(spectra_width, "rows", split_axis=3, concat_axis=2, tiled=True)
    )
    slab_width = columns.shape[3]
    offset = lax.axis_index("rows") * slab_width
    freq_height = frequencies(jnp.arange(N, dtype=jnp.int32))
    freq_width = frequencies(offset + jnp.arange(slab_width, dtype=jnp.int32))
    radical = jnp.sqrt(4.0 - freq_height[:, None] ** 2 - freq_width[None, :] ** 2)
    distance = 100.0 + 2.0 * depth_index.astype(jnp.float32)
    phases = (2.0 * math.pi * distance)[:, None, None] * (radical - 2.0)[None, :, :]
    ordered = reorder_mask(band_mask)
    mask_height = ordered[:, 0, :].astype(jnp.float32)
    mask_width = lax.dynamic_slice_in_dim(ordered[:, 1, :], offset, slab_width, 1).astype(
        jnp.float32
    )
    weights = mask_height[:, :, None] * mask_width[:, None, :]
    cosine = jnp.cos(phases) * weights
    sine_part = jnp.sin(phases) * weights
    real_part = columns[:, 0]
    imaginary_part = columns[:, 1]
    spectrum = jnp.stack(
        [
            jnp.sum(real_part * cosine - imaginary_part * sine_part, axis=0),
            jnp.sum(real_part * sine_part + imaginary_part * cosine, axis=0),
        ]
    )
    scaling = 1.0 / math.sqrt(plane_count * lax.axis_size("depth"))
    field_part = inverse_height(spectrum)
    shares = lax.psum_scatter(field_part, "depth", scatter_dimension=1, tiled=True)
    rows_out = lax.all_to_all(shares, "rows", split_axis=1, concat_axis=2, tiled=True)
    return inverse_width(rows_out) * scaling


def solution(mesh):
    in_specs = (P("depth", None, "rows", None), P("depth"), P("depth", None, None))
    out_specs = P(None, ("depth", "rows"), None)
    return jax.shard_map(local, mesh=mesh, in_specs=in_specs, out_specs=out_specs, check_vma=False)
```

profile of v0, /device:TPU:0, one launch (start us, length us, event | category | flops | bytes accessed | tf_op | source)
XLA Modules:
  0.0 982.7 jit_solution(7739893141141795553)
XLA Ops:
  6.5 0.1 multiply_sine_fusion.2
  6.7 0.1 sine_multiply_fusion.1
  6.8 0.3 multiply_sine_fusion.1
  7.1 0.3 fusion.49
  7.3 14.1 %copy.117 = f32[128,8,32,128]{3,2,1,0:T(8,128)} copy(f32[128,8,32,128]{3,1,2,0:T(8,128)} %bitcast.227) | data formatting | bytes 33554432
  21.4 22.1 %fusion.24 = f32[1,2,512,32,128]{4,3,2,1,0:T(8,128)} fusion(f32[1,32,2,32]{3,1,2,0:T(8,128)S(1)} %get-tuple-element.122, f32[1,32,2,32]{3,1,2,0:T(8,128)S(1)} %get-tuple-element.121, f32[2,512,32,128]{3,2,1,0:T(8,128)} %bitcast.219), kind=kOutput, calls=%fused_computation.39 | convolution fusion | flops 3221229568 | bytes 33570816 | tf_op jit(solution)/shard_map/akbn,pbrnm->parkm/dot_general | solution.py:49
  43.6 7.2 subtract_bitcast_fusion.2
  50.7 6.2 maximum_bitcast_fusion
  56.9 42.9 %fusion.14 = f32[1,2,512,32,128]{2,4,1,3,0:T(8,128)} fusion(f32[2,512,32,128,1]{3,2,1,0,4:T(8,128)} %maximum_bitcast_fusion, f32[1,128,2,128]{3,1,2,0:T(8,128)S(1)} %get-tuple-element.116, f32[1,128,2,128]{3,1,2,0:T(8,128)S(1)} %get-tuple-element.115), kind=kOutput, calls=%fused_computation.20 | convolution fusion | flops 12884967424 | bytes 33816576 | tf_op jit(solution)/shard_map/akbn,pbrjn->parjk/dot_general | solution.py:51
  99.9 6.9 copy.63
  106.7 32.2 %copy.64 = f32[1,2,512,4096]{2,1,0,3:T(2,128)} copy(f32[1,2,512,4096]{2,3,1,0:T(8,128)S(1)} %bitcast.223) | data formatting | bytes 33554432 | tf_op jit(solution)/shard_map/reshape | solution.py:52
  139.0 5.9 all-to-all-start
  144.9 0.1 copy.69
  145.0 0.1 copy.70
  145.1 0.1 reshape.712
  146.2 0.1 sine_multiply_fusion
  146.3 0.1 multiply_sine_fusion.3
  146.3 0.3 fusion.50
  146.6 0.3 multiply_sine_fusion
  146.9 182.5 %all-to-all-done = f32[1,2,512,4096]{2,1,0,3:T(2,128)} async-done(((f32[1,2,512,4096]{2,1,0,3:T(2,128)}), f32[1,2,512,4096]{2,1,0,3:T(2,128)}, u32[]{:S(2)}, u32[]{:S(2)}) %all-to-all-start) | async-done | bytes 16777248 | tf_op jit(solution)/shard_map/all_to_all | solution.py:103
  329.4 14.1 %copy.65 = f32[1,2,512,4096]{2,3,1,0:T(8,128)} copy(f32[1,2,512,4096]{2,1,0,3:T(2,128)} %all-to-all-done) | data formatting | bytes 33554432 | tf_op jit(solution)/shard_map/all_to_all | solution.py:103
  343.5 17.3 %copy.66 = f32[1,2,8,512,512]{4,3,2,1,0:T(8,128)} copy(f32[1,2,8,512,512]{3,4,2,1,0:T(8,128)} %bitcast.224) | data formatting | bytes 33554432 | tf_op jit(solution)/shard_map/all_to_all | solution.py:103
  360.8 32.4 %fusion.17 = f32[1,2,32,128,512]{4,2,1,3,0:T(8,128)S(1)} fusion(f32[2,32,128,512,1]{3,2,1,0,4:T(8,128)} %bitcast.220, f32[1,32,2,32]{3,1,2,0:T(8,128)S(1)} %get-tuple-element.122, f32[1,32,2,32]{3,1,2,0:T(8,128)S(1)} %get-tuple-element.121), kind=kOutput, calls=%fused_computation.21 | convolution fusion | flops 3221229568 | bytes 33570816 | tf_op jit(solution)/shard_map/akbn,pbnjs->pakjs/dot_general | solution.py:59
  393.2 4.5 subtract_bitcast_fusion.1
  397.7 4.9 maximum_bitcast_fusion.1
  402.6 27.0 %fusion.20 = f32[1,2,32,128,512]{4,3,1,2,0:T(8,128)S(1)} fusion(f32[2,32,128,512,1]{3,1,2,0,4:T(8,128)S(1)} %maximum_bitcast_fusion.1, f32[1,128,2,128]{3,1,2,0:T(8,128)S(1)} %get-tuple-element.116, f32[1,128,2,128]{3,1,2,0:T(8,128)S(1)} %get-tuple-element.115), kind=kOutput, calls=%fused_computation.22 | convolution fusion | flops 12884967424 | bytes 33816576 | tf_op jit(solution)/shard_map/akbn,pbjns->pajks/dot_general | solution.py:61
  429.6 6.2 copy.72
  435.8 10.9 %fusion.86 = (f32[1,1,4096,512]{3,2,1,0:T(8,128)}, f32[1,1,4096,512]{3,2,1,0:T(8,128)}) fusion(f32[1,2,4096,512]{3,2,1,0:T(8,128)} %bitcast.222), kind=kLoop, calls=%fused_computation.148 | loop fusion | bytes 33554432 | tf_op jit(solution)/shard_map/slice | solution.py:120
  446.7 9.0 copy.74
  455.7 9.0 copy.75
  464.7 37.7 %multiply_subtract_fusion = (f32[1,32,128,512]{2,3,0,1:T(8,128)S(1)}, f32[1,32,128,512]{2,3,0,1:T(8,128)}) fusion(f32[1,32,128,512]{2,3,0,1:T(8,128)} %copy.75, f32[1,32,128,512]{2,3,0,1:T(8,128)} %copy.74, f32[512]{0:T(512)S(1)} %bitcast.233, f32[32,128]{1,0:T(8,128)S(1)} %bitcast.232, f32[512]{0:T(512)S(1)} %multiply_multiply_fusion.2, ...), kind=kLoop, calls=%fused_computation.33 | loop fusion | flops 25165824 | bytes 33591300 | tf_op jit(solution)/shard_map/sub | solution.py:124
  502.4 16.5 %fusion.23 = f32[2,32,128,512]{2,3,0,1:T(8,128)S(1)} fusion(f32[1,32,128,512]{2,3,0,1:T(8,128)} %get-tuple-element.104, f32[1,32,128,512]{2,3,0,1:T(8,128)S(1)} %get-tuple-element.103, f32[1,128,2,128]{3,1,2,0:T(8,128)S(1)} %get-tuple-element.114, f32[1,128,2,128]{3,1,2,0:T(8,128)S(1)} %get-tuple-element.113), kind=kOutput, calls=%fused_computation.23 | convolution fusion | flops 12889161728 | bytes 33816576 | tf_op jit(solution)/shard_map/anbk,bjks->ajns/dot_general | solution.py:69
  518.9 6.9 subtract_bitcast_fusion
  525.8 11.5 %pad_maximum_fusion = f32[2,32,128,512]{2,3,1,0:T(8,128)} fusion(f32[1,32,128,512]{2,3,1,0:T(8,128)} %get-tuple-element.106, f32[1,32,128,512]{2,3,1,0:T(8,128)} %get-tuple-element.105), kind=kLoop, calls=%fused_computation.6 | loop fusion | flops 4194304 | bytes 33554432 | tf_op jit(solution)/shard_map/stack | solution.py:36
  537.3 19.9 %copy.79 = f32[2,32,128,512]{3,1,0,2:T(8,128)} copy(f32[2,32,128,512]{2,3,1,0:T(8,128)} %pad_maximum_fusion) | data formatting | bytes 33554432 | tf_op jit(solution)/shard_map/stack | solution.py:36
  557.2 21.8 %fusion.27 = f32[2,32,128,512]{3,1,2,0:T(8,128)} fusion(f32[2,32,128,512]{3,1,0,2:T(8,128)} %copy.79, f32[1,32,2,32]{3,1,2,0:T(8,128)S(1)} %get-tuple-element.120, f32[1,32,2,32]{3,1,2,0:T(8,128)S(1)} %get-tuple-element.119), kind=kOutput, calls=%fused_computation.40 | convolution fusion | flops 3221229568 | bytes 33570816 | tf_op jit(solution)/shard_map/anbk,bkjs->anjs/dot_general | solution.py:71
  579.0 17.9 %copy.80 = f32[2,32,128,512]{3,2,1,0:T(8,128)} copy(f32[2,32,128,512]{3,1,2,0:T(8,128)} %fusion.27) | data formatting | bytes 33554432 | tf_op jit(solution)/shard_map/anbk,bkjs->anjs/dot_general | solution.py:71
  596.9 280.8 %reduce-scatter.2.cloned.1.call-done = f32[2,1024,512]{2,1,0:T(8,128)} async-done(((f32[2,4096,512]{2,1,0:T(8,128)}), f32[2,1024,512]{2,1,0:T(8,128)}) %reduce-scatter.2.cloned.1.call-update) | async-done | bytes 4194320 | tf_op jit(solution)/shard_map/reduce_scatter | solution.py:130
  877.7 5.4 copy.81
  883.1 52.5 %all_to_all.30 = f32[2,1024,512]{2,0,1:T(2,128)S(1)} all-to-all(f32[2,1024,512]{2,0,1:T(2,128)S(1)} %copy.81), channel_id=1, replica_groups=mesh['depth'=4,'rows'=8] {'rows'}, dimensions={1} | all-to-all | bytes 8388608 | tf_op jit(solution)/shard_map/all_to_all | solution.py:131
  935.6 2.8 copy.82
  938.4 5.3 copy.83
  943.8 8.5 fusion.35
  952.3 0.9 subtract_bitcast_fusion.3
  953.2 0.5 maximum_bitcast_fusion.6
  953.7 9.0 fusion.30
  962.7 6.0 mul.976
  968.8 6.6 copy.87
  (15 shorter events, 0.4 us)
Async XLA Ops:
  139.0 6.1 copy-start
  139.0 190.5 %all-to-all-start = ((f32[1,2,512,4096]{2,1,0,3:T(2,128)}), f32[1,2,512,4096]{2,1,0,3:T(2,128)}, u32[]{:S(2)}, u32[]{:S(2)}) async-start(f32[1,2,512,4096]{2,1,0,3:T(2,128)} %copy.64), calls=%async_computation | async-start | bytes 33554432 | tf_op jit(solution)/shard_map/all_to_all | solution.py:103
  144.9 732.9 %reduce-scatter.2.cloned.1.call-start = ((), (), s32[]{:S(2)}) async-start(), calls=%async_computation.3 | async-start | bytes 20971520 | tf_op jit(solution)/shard_map/reduce_scatter | solution.py:130
Sparse Core Ops, SparseCore 0:
  597.0 280.6 reduce-scatter.1
where the time goes:
time: 993 us; the launch traced here: 983 us
  waiting for transfers between devices  463 us (47%)
  local copies, waits for them, and re-layouts  184 us (19%)
  matrix products  180 us (18%)
  other arithmetic  81.9 us (8%)
  blocking collectives  52.5 us (5%)
  between operations  14.7 us (1%)
    reduce_scatter x1, waiting for transfers between devices, local(): lax.psum_scatter(field_part, 'depth', scatter_dimension=1, tiled=True)  281 us
    all_to_all x1, waiting for transfers between devices, local(): lax.all_to_all(spectra_width, 'rows', split_axis=3, concat_axis=2, tiled=...  183 us
    all_to_all x1, blocking collectives, local(): lax.all_to_all(shares, 'rows', split_axis=1, concat_axis=2, tiled=True)  52.5 us
    dot_general x1, matrix products, along_width(): jnp.einsum('akbn,pbrjn->parjk', block_table(HIGH, -1.0), turned, precisio...  42.9 us
    sub x1, other arithmetic, local(): real_part * cosine - imaginary_part * sine_part  37.7 us
    dot_general x1, matrix products, along_height(): jnp.einsum('akbn,pbnjs->pakjs', block_table(LOW, -1.0), pieces, precision...  32.4 us
    reshape x1, local copies, waits for them, and re-layouts, along_width(): return result.reshape(plane_count, 2, height, N)  32.2 us
    another operation x6, other arithmetic, rotate_pair(): jnp.stack([real_part * factor_real - imaginary_part * factor_imaginary, r...  31.4 us
  transfers between devices with their start and end apart: 2, of which 2 were waited for; matrix products, arithmetic and copies ran while one was open for 0% of the time, Pallas kernels for 0%

commit v1 on v0

--- a/solution.py
+++ b/solution.py
@@ -8,6 +8,13 @@
 HIGH = 128
 N = 4096
 precise = lax.Precision.HIGHEST
+
+
+def stacked_exchange(array, mesh_axis, split, join):
+    peers = lax.axis_size(mesh_axis)
+    blocks = jnp.stack(jnp.split(array, peers, axis=split), axis=0)
+    blocks = lax.all_to_all(blocks, mesh_axis, split_axis=0, concat_axis=0)
+    return jnp.concatenate(blocks, axis=join)
 
 
 def block_table(length, direction):
@@ -99,9 +106,7 @@
 def local(target, depth_index, band_mask):
     plane_count = target.shape[0]
     spectra_width = along_width(target)
-    columns = along_height(
-        lax.all_to_all(spectra_width, "rows", split_axis=3, concat_axis=2, tiled=True)
-    )
+    columns = along_height(stacked_exchange(spectra_width, "rows", 3, 2))
     slab_width = columns.shape[3]
     offset = lax.axis_index("rows") * slab_width
     freq_height = frequencies(jnp.arange(N, dtype=jnp.int32))

time: 993 us -> 950 us (0.957)
  local copies, waits for them, and re-layouts: 184 us -> 151 us
    all_to_all x2 -> x0, local copies, waits for them, and re-layouts: 31.4 us -> none  [local(): lax.all_to_all(spectra_width, 'rows', split_axis=3, concat_axis=2, tiled=...]
    reshape x1, local copies, waits for them, and re-layouts: 32.2 us -> 17.6 us  [stacked_exchange(): return jnp.concatenate(blocks, axis=join)]
    unnamed x3 -> x10, local copies, waits for them, and re-layouts: 14.1 us -> 24.7 us
where the time goes in v1:
time: 950 us; the launch traced here: 940 us
  waiting for transfers between devices  463 us (49%)
  matrix products  171 us (18%)
  local copies, waits for them, and re-layouts  151 us (16%)
  other arithmetic  81.9 us (9%)
  blocking collectives  52.5 us (6%)
  between operations  14.7 us (2%)
    reduce_scatter x1, waiting for transfers between devices, local(): lax.psum_scatter(field_part, 'depth', scatter_dimension=1, tiled=True)  281 us
    all_to_all x1, waiting for transfers between devices, stacked_exchange(): blocks = lax.all_to_all(blocks, mesh_axis, split_axis=0, concat_axis=0)  183 us
    all_to_all x1, blocking collectives, local(): lax.all_to_all(shares, 'rows', split_axis=1, concat_axis=2, tiled=True)  52.5 us
    sub x1, other arithmetic, local(): real_part * cosine - imaginary_part * sine_part  37.7 us
    dot_general x1, matrix products, along_width(): jnp.einsum('akbn,pbrjn->parjk', block_table(HIGH, -1.0), turned, precisio...  33.2 us
    dot_general x1, matrix products, along_height(): jnp.einsum('akbn,pbnjs->pakjs', block_table(LOW, -1.0), pieces, precision...  32.4 us
    another operation x6, other arithmetic, rotate_pair(): jnp.stack([real_part * factor_real - imaginary_part * factor_imaginary, r...  31.4 us
    dot_general x1, matrix products, along_height(): jnp.einsum('akbn,pbjns->pajks', block_table(HIGH, -1.0), turned, precisio...  27 us
  transfers between devices with their start and end apart: 2, of which 2 were waited for; matrix products, arithmetic and copies ran while one was open for 0% of the time, Pallas kernels for 0%

profile of v1, /device:TPU:0, one launch (start us, length us, event | category | flops | bytes accessed | tf_op | source)
XLA Modules:
  0.0 939.6 jit_solution(18001811838296417870)
XLA Ops:
  6.8 0.3 multiply_sine_fusion.1
  7.1 0.3 fusion.57
  7.3 14.1 %copy.115 = f32[128,8,32,128]{3,2,1,0:T(8,128)} copy(f32[128,8,32,128]{3,1,2,0:T(8,128)} %bitcast.263) | data formatting | bytes 33554432
  21.4 22.1 %fusion.24 = f32[1,2,512,32,128]{4,3,2,1,0:T(8,128)} fusion(f32[1,32,2,32]{3,1,2,0:T(8,128)S(1)} %get-tuple-element.122, f32[1,32,2,32]{3,1,2,0:T(8,128)S(1)} %get-tuple-element.121, f32[2,512,32,128]{3,2,1,0:T(8,128)} %bitcast.249), kind=kOutput, calls=%fused_computation.39 | convolution fusion | flops 3221229568 | bytes 33570816 | tf_op jit(solution)/shard_map/akbn,pbrnm->parkm/dot_general | solution.py:56
  43.6 7.2 subtract_bitcast_fusion.2
  50.7 6.2 maximum_bitcast_fusion
  56.9 33.2 %fusion.14 = f32[1,2,512,32,128]{2,4,1,3,0:T(8,128)} fusion(f32[2,512,32,128,1]{3,2,1,0,4:T(8,128)} %maximum_bitcast_fusion, f32[1,128,2,128]{3,1,2,0:T(8,128)S(1)} %get-tuple-element.116, f32[1,128,2,128]{3,1,2,0:T(8,128)S(1)} %get-tuple-element.115), kind=kOutput, calls=%fused_computation.20 | convolution fusion | flops 12884967424 | bytes 33816576 | tf_op jit(solution)/shard_map/akbn,pbrjn->parjk/dot_general | solution.py:58
  90.2 7.4 copy.63
  97.6 1.5 fusion.47
  99.1 1.5 fusion.46
  100.6 1.5 fusion.45
  102.1 1.5 fusion.44
  103.6 1.6 fusion.43
  105.2 1.5 fusion.42
  106.7 1.5 fusion.41
  108.2 1.5 fusion.40
  109.7 5.9 all-to-all-start
  115.8 0.1 reshape.714
  117.0 0.3 fusion.58
  117.3 0.3 multiply_sine_fusion
  117.6 182.5 %all-to-all-done = f32[8,1,2,512,512]{3,4,2,1,0:T(8,128)} async-done(((f32[8,1,2,512,512]{3,4,2,1,0:T(8,128)}), f32[8,1,2,512,512]{3,4,2,1,0:T(8,128)}, u32[]{:S(2)}, u32[]{:S(2)}) %all-to-all-start) | async-done | bytes 16777248 | tf_op jit(solution)/shard_map/all_to_all | solution.py:16
  300.1 17.6 %copy.64 = f32[1,2,8,512,512]{4,3,2,1,0:T(8,128)} copy(f32[1,2,8,512,512]{3,4,1,0,2:T(8,128)} %bitcast.39) | data formatting | bytes 33554432 | tf_op jit(solution)/shard_map/reshape | solution.py:17
  317.7 32.4 %fusion.17 = f32[1,2,32,128,512]{4,2,1,3,0:T(8,128)S(1)} fusion(f32[2,32,128,512,1]{3,2,1,0,4:T(8,128)} %bitcast.250, f32[1,32,2,32]{3,1,2,0:T(8,128)S(1)} %get-tuple-element.122, f32[1,32,2,32]{3,1,2,0:T(8,128)S(1)} %get-tuple-element.121), kind=kOutput, calls=%fused_computation.21 | convolution fusion | flops 3221229568 | bytes 33570816 | tf_op jit(solution)/shard_map/akbn,pbnjs->pakjs/dot_general | solution.py:66
  350.1 4.5 subtract_bitcast_fusion.1
  354.6 4.9 maximum_bitcast_fusion.1
  359.5 27.0 %fusion.20 = f32[1,2,32,128,512]{4,3,1,2,0:T(8,128)S(1)} fusion(f32[2,32,128,512,1]{3,1,2,0,4:T(8,128)S(1)} %maximum_bitcast_fusion.1, f32[1,128,2,128]{3,1,2,0:T(8,128)S(1)} %get-tuple-element.116, f32[1,128,2,128]{3,1,2,0:T(8,128)S(1)} %get-tuple-element.115), kind=kOutput, calls=%fused_computation.22 | convolution fusion | flops 12884967424 | bytes 33816576 | tf_op jit(solution)/shard_map/akbn,pbjns->pajks/dot_general | solution.py:68
  386.5 6.2 copy.70
  392.7 10.9 %fusion.94 = (f32[1,1,4096,512]{3,2,1,0:T(8,128)}, f32[1,1,4096,512]{3,2,1,0:T(8,128)}) fusion(f32[1,2,4096,512]{3,2,1,0:T(8,128)} %bitcast.260), kind=kLoop, calls=%fused_computation.164 | loop fusion | bytes 33554432 | tf_op jit(solution)/shard_map/slice | solution.py:125
  403.6 9.0 copy.72
  412.6 9.0 copy.73
  421.6 37.7 %multiply_subtract_fusion = (f32[1,32,128,512]{2,3,0,1:T(8,128)S(1)}, f32[1,32,128,512]{2,3,0,1:T(8,128)}) fusion(f32[1,32,128,512]{2,3,0,1:T(8,128)} %copy.73, f32[1,32,128,512]{2,3,0,1:T(8,128)} %copy.72, f32[512]{0:T(512)S(1)} %bitcast.269, f32[32,128]{1,0:T(8,128)S(1)} %bitcast.268, f32[512]{0:T(512)S(1)} %multiply_multiply_fusion.2, ...), kind=kLoop, calls=%fused_computation.33 | loop fusion | flops 25165824 | bytes 33591300 | tf_op jit(solution)/shard_map/sub | solution.py:129
  459.3 16.5 %fusion.23 = f32[2,32,128,512]{2,3,0,1:T(8,128)S(1)} fusion(f32[1,32,128,512]{2,3,0,1:T(8,128)} %get-tuple-element.104, f32[1,32,128,512]{2,3,0,1:T(8,128)S(1)} %get-tuple-element.103, f32[1,128,2,128]{3,1,2,0:T(8,128)S(1)} %get-tuple-element.114, f32[1,128,2,128]{3,1,2,0:T(8,128)S(1)} %get-tuple-element.113), kind=kOutput, calls=%fused_computation.23 | convolution fusion | flops 12889161728 | bytes 33816576 | tf_op jit(solution)/shard_map/anbk,bjks->ajns/dot_general | solution.py:76
  475.8 6.9 subtract_bitcast_fusion
  482.7 11.5 %pad_maximum_fusion = f32[2,32,128,512]{2,3,1,0:T(8,128)} fusion(f32[1,32,128,512]{2,3,1,0:T(8,128)} %get-tuple-element.106, f32[1,32,128,512]{2,3,1,0:T(8,128)} %get-tuple-element.105), kind=kLoop, calls=%fused_computation.6 | loop fusion | flops 4194304 | bytes 33554432 | tf_op jit(solution)/shard_map/stack | solution.py:43
  494.2 19.9 %copy.77 = f32[2,32,128,512]{3,1,0,2:T(8,128)} copy(f32[2,32,128,512]{2,3,1,0:T(8,128)} %pad_maximum_fusion) | data formatting | bytes 33554432 | tf_op jit(solution)/shard_map/stack | solution.py:43
  514.1 21.8 %fusion.27 = f32[2,32,128,512]{3,1,2,0:T(8,128)} fusion(f32[2,32,128,512]{3,1,0,2:T(8,128)} %copy.77, f32[1,32,2,32]{3,1,2,0:T(8,128)S(1)} %get-tuple-element.120, f32[1,32,2,32]{3,1,2,0:T(8,128)S(1)} %get-tuple-element.119), kind=kOutput, calls=%fused_computation.40 | convolution fusion | flops 3221229568 | bytes 33570816 | tf_op jit(solution)/shard_map/anbk,bkjs->anjs/dot_general | solution.py:78
  535.9 17.9 %copy.78 = f32[2,32,128,512]{3,2,1,0:T(8,128)} copy(f32[2,32,128,512]{3,1,2,0:T(8,128)} %fusion.27) | data formatting | bytes 33554432 | tf_op jit(solution)/shard_map/anbk,bkjs->anjs/dot_general | solution.py:78
  553.8 280.8 %reduce-scatter.2.cloned.1.call-done = f32[2,1024,512]{2,1,0:T(8,128)} async-done(((f32[2,4096,512]{2,1,0:T(8,128)}), f32[2,1024,512]{2,1,0:T(8,128)}) %reduce-scatter.2.cloned.1.call-update) | async-done | bytes 4194320 | tf_op jit(solution)/shard_map/reduce_scatter | solution.py:135
  834.6 5.4 copy.79
  840.0 52.5 %all_to_all.20 = f32[2,1024,512]{2,0,1:T(2,128)S(1)} all-to-all(f32[2,1024,512]{2,0,1:T(2,128)S(1)} %copy.79), channel_id=1, replica_groups=mesh['depth'=4,'rows'=8] {'rows'}, dimensions={1} | all-to-all | bytes 8388608 | tf_op jit(solution)/shard_map/all_to_all | solution.py:136
  892.5 2.8 copy.80
  895.3 5.3 copy.81
  900.6 8.5 fusion.35
  909.2 0.9 subtract_bitcast_fusion.3
  910.1 0.5 maximum_bitcast_fusion.6
  910.6 9.0 fusion.30
  919.6 6.0 mul.976
  925.6 6.6 copy.85
  (21 shorter events, 1.0 us)
Async XLA Ops:
  109.7 6.1 copy-start
  109.7 190.5 %all-to-all-start = ((f32[8,1,2,512,512]{3,4,2,1,0:T(8,128)}), f32[8,1,2,512,512]{3,4,2,1,0:T(8,128)}, u32[]{:S(2)}, u32[]{:S(2)}) async-start(f32[8,1,2,512,512]{3,4,2,1,0:T(8,128)} %fusion.40), calls=%async_computation | async-start | bytes 33554432 | tf_op jit(solution)/shard_map/all_to_all | solution.py:16
  115.5 719.1 %reduce-scatter.2.cloned.1.call-start = ((), (), s32[]{:S(2)}) async-start(), calls=%async_computation.3 | async-start | bytes 20971520 | tf_op jit(solution)/shard_map/reduce_scatter | solution.py:135
Sparse Core Ops, SparseCore 0:
  553.9 280.6 reduce-scatter.1
